TPU v7x, 32 devices: a whole 2x2x4 slice. The times are simulated.
32 devices in a mesh: gx: 8 (over z, x), gy: 4 (over y, core).
Axes of the slice: x: 2, y: 2, z: 4, core: 2. Of those that a mesh axis runs over, the one named last changes fastest.
Arguments:
- source_tiles: bfloat16 [96, 32, 192, 384], P(('gx', 'gy')), may hold values from -6 to 6
- tile_offsets: int32 [2, 96], P(None, ('gx', 'gy')), may hold values from -128 to 896, as said below
- tile_shifts: int32 [96], P(('gx', 'gy')), may hold values from 0 to 63
- tile_counts: int32 [32], P(('gx', 'gy')), may hold values from 1 to 3, as said below
Outputs:
- merged_slab: float32 [32, 1024, 1024], P(None, 'gx', 'gy')
Inputs may be any that keep to these rules, and one draw needn't show every extreme that they name: `tile_offsets`: slot k belongs to the device of joined gx+gy index d = k // 3, that is gx index d // 4 and gy index d % 4. Its x offset lies from that gx index times 128 minus 64 up to that gx index times 128; its y offset from the gy index times 256 minus 128 up to the gy index times 256. So every tile covers its owner's whole block. `tile_counts`: entry d counts the used slots of device d; they are its first slots, the others are ignored. Both 1 and 3 occur in every draw.
All inputs are finite; a program needn't handle non-finite values.
Results may differ from a plain program's by a relative error of at most 0.0003.
Values sent between devices are 32-bit elements; how exact they have to be, the bound alone decides.
A program may use at most 192 MiB of HBM per device.

v0:
```python
import functools

import jax
import jax.numpy as jnp
from jax import lax
from jax.experimental import pallas as pl
from jax.experimental.pallas import tpu as pltpu
from jax.sharding import PartitionSpec as P

BX = 128
BY = 256
RAMP = 32
RX = 64
RY = 128
LAG_Y = 2
LAG_X = 10
MESH = pl.DeviceIdType.MESH


def ramp_at(place, length):
    place = place.astype(jnp.float32)
    ramp = jnp.minimum(jnp.minimum(place + 1.0, length - place), float(RAMP))
    return jnp.where((place >= 0) & (place < length), ramp, 0.0)


def band(starts, fractions, length, extent):
    target = jnp.arange(extent, dtype=jnp.int32)[None, :, None] - starts[:, None, None]
    source = jnp.arange(length, dtype=jnp.int32)[None, None, :]
    fraction = fractions[:, None, None]
    here = jnp.where(source == target, 1.0 - fraction, 0.0)
    after = jnp.where(source == jnp.minimum(target + 1, length - 1), fraction, 0.0)
    return ramp_at(target, length) * (here + after)


def kernel(
    grid_x, grid_y, depth_ref, first_ref, next_ref, across_ref, along_ref, wide_x_ref, wide_y_ref,
    out_ref, centre, up, down, above, below, from_left, from_right, held, parts, scale,
    up_sent, down_sent, left_sent, right_sent, above_sem, below_sem, from_left_sem, from_right_sem,
):
    slots, length = first_ref.shape[0], first_ref.shape[2]
    half = along_ref.shape[2] // 2
    count = centre.shape[0]
    step = pl.program_id(0)
    column, row = lax.axis_index("gx"), lax.axis_index("gy")
    has_left, has_right = column > 0, column < grid_x - 1
    has_below, has_above = row > 0, row < grid_y - 1
    to_left, to_right = (column - 1, row), (column + 1, row)
    to_below, to_above = (column, row - 1), (column, row + 1)

    def remote(source, target, sent, arrived, device):
        return pltpu.make_async_remote_copy(
            src_ref=source, dst_ref=target, send_sem=sent, recv_sem=arrived,
            device_id=device, device_id_type=MESH,
        )

    def copy_below(n):
        return remote(up.at[n], above.at[n], up_sent.at[n], above_sem.at[n], to_below)

    def copy_above(n):
        return remote(down.at[n], below.at[n], down_sent.at[n], below_sem.at[n], to_above)

    def copy_left(n):
        return remote(
            centre.at[n, pl.ds(0, RX)], from_right.at[n], left_sent.at[n], from_right_sem.at[n], to_left
        )

    def copy_right(n):
        return remote(
            centre.at[n, pl.ds(RX + BX, RX)], from_left.at[n], right_sent.at[n], from_left_sem.at[n],
            to_right,
        )

    def along(plane, k):
        low = jnp.dot(plane, along_ref[k, :, :half], preferred_element_type=jnp.float32)
        cut = half - RY
        high = jnp.dot(
            plane[:, cut:], along_ref[k, cut:, half:], preferred_element_type=jnp.float32
        )
        return low, high

    def split(total):
        up[step] = total[:, :RY]
        centre[step] = total[:, RY : RY + BY]
        down[step] = total[:, RY + BY :]

    @pl.when(step == 0)
    def _():
        barrier = pltpu.get_barrier_semaphore()
        for there, device in (
            (has_left, to_left), (has_right, to_right), (has_below, to_below), (has_above, to_above)
        ):
            @pl.when(there)
            def _():
                pl.semaphore_signal(barrier, inc=1, device_id=device, device_id_type=MESH)

        split(jnp.dot(wide_x_ref[...], wide_y_ref[...], preferred_element_type=jnp.float32))
        for k in range(slots):
            low, high = along(first_ref[k, 0], k)
            held[k, :, :half] = low
            held[k, :, half:] = high
        peers = [jnp.where(there, 1, 0) for there in (has_left, has_right, has_below, has_above)]
        pl.semaphore_wait(barrier, sum(peers))

    @pl.when((step > 0) & (step < count))
    def _():
        for k in range(slots):
            fraction = depth_ref[k]
            for number, later in enumerate(along(next_ref[k, 0], k)):
                lanes = slice(number * half, (number + 1) * half)
                mixed = held[k, :, lanes] * (1.0 - fraction) + later * fraction
                held[k, :, lanes] = later
                top = mixed.astype(jnp.bfloat16)
                rest = (mixed - top.astype(jnp.float32)).astype(jnp.bfloat16)
                parts[2 * k * length : (2 * k + 1) * length, lanes] = top
                parts[(2 * k + 1) * length : (2 * k + 2) * length, lanes] = rest
        split(jnp.dot(across_ref[...], parts[...], preferred_element_type=jnp.float32))

    @pl.when(step < count)
    def _():
        @pl.when(has_below)
        def _():
            copy_below(step).start()

        @pl.when(has_above)
        def _():
            copy_above(step).start()

    @pl.when((step >= LAG_Y) & (step < count + LAG_Y))
    def _():
        n = step - LAG_Y

        @pl.when(has_below)
        def _():
            copy_above(n).wait_recv()
            centre[n, :, :RY] += below[n]

        @pl.when(has_above)
        def _():
            copy_below(n).wait_recv()
            centre[n, :, RY:] += above[n]

        @pl.when(has_left)
        def _():
            copy_left(n).start()

        @pl.when(has_right)
        def _():
            copy_right(n).start()

    @pl.when(step >= LAG_X)
    def _():
        n = step - LAG_X

        @pl.when(has_left)
        def _():
            copy_right(n).wait_recv()
            centre[n, RX : 2 * RX] += from_left[n]
            copy_left(n).wait_send()

        @pl.when(has_right)
        def _():
            copy_left(n).wait_recv()
            centre[n, BX : BX + RX] += from_right[n]
            copy_right(n).wait_send()

        @pl.when(has_below)
        def _():
            copy_below(n).wait_send()

        @pl.when(has_above)
        def _():
            copy_above(n).wait_send()

        @pl.when(n == 0)
        def _():
            scale[...] = 1.0 / jnp.maximum(centre[n, RX : RX + BX], 1.0)

        @pl.when(n > 0)
        def _():
            out_ref[0] = centre[n, RX : RX + BX] * scale[...]


def merged(grid_x, grid_y, depth, tiles, across, along, wide_x, wide_y):
    slots, depth_cells, length, rows = tiles.shape
    count = depth_cells + 1
    extent_x, extent_y = across.shape[0], along.shape[2]
    plane = (slots, 1, length, rows)
    slab = lambda *shape: pltpu.VMEM((count,) + shape, jnp.float32)
    return pl.pallas_call(
        functools.partial(kernel, grid_x, grid_y),
        grid=(count + LAG_X,),
        in_specs=[
            pl.BlockSpec(memory_space=pltpu.SMEM),
            pl.BlockSpec(plane, lambda s: (0, 0, 0, 0)),
            pl.BlockSpec(plane, lambda s: (0, jnp.clip(s, 1, depth_cells - 1), 0, 0)),
            pl.BlockSpec(across.shape, lambda s: (0, 0)),
            pl.BlockSpec(along.shape, lambda s: (0, 0, 0)),
            pl.BlockSpec(wide_x.shape, lambda s: (0, 0)),
            pl.BlockSpec(wide_y.shape, lambda s: (0, 0)),
        ],
        out_specs=pl.BlockSpec((1, BX, BY), lambda s: (jnp.maximum(s - LAG_X - 1, 0), 0, 0)),
        out_shape=jax.ShapeDtypeStruct((depth_cells, BX, BY), jnp.float32),
        scratch_shapes=[
            slab(extent_x, BY),
            slab(extent_x, RY),
            slab(extent_x, RY),
            slab(extent_x, RY),
            slab(extent_x, RY),
            slab(RX, BY),
            slab(RX, BY),
            pltpu.VMEM((slots, length, extent_y), jnp.float32),
            pltpu.VMEM((2 * slots * length, extent_y), jnp.bfloat16),
            pltpu.VMEM((BX, BY), jnp.float32),
        ]
        + [pltpu.SemaphoreType.DMA((count,))] * 8,
        compiler_params=pltpu.CompilerParams(
            collective_id=0, has_side_effects=True, vmem_limit_bytes=60 * 1024 * 1024,
            dimension_semantics=("arbitrary",),
        ),
        name="merged",
    )(depth, tiles, tiles, across, along, wide_x, wide_y)


def local(grid_x, grid_y, source_tiles, tile_offsets, tile_shifts, tile_counts):
    slots, depth_cells, length, rows = source_tiles.shape
    starts_x = tile_offsets[0] - lax.axis_index("gx") * BX + RX
    starts_y = tile_offsets[1] - lax.axis_index("gy") * BY + RY
    active = (jnp.arange(slots) < tile_counts[0]).astype(jnp.float32)
    depth_part = (tile_shifts // 16 % 4).astype(jnp.float32) * 0.25
    column_part = (tile_shifts // 4 % 4).astype(jnp.float32) * 0.25
    row_part = (tile_shifts % 4).astype(jnp.float32) * 0.25
    across = band(starts_x, column_part, length, BX + 2 * RX) * active[:, None, None]
    across = jnp.concatenate([across[k] for k in range(slots) for part in (0, 1)], axis=1)
    across = across.astype(jnp.bfloat16)
    along = band(starts_y, row_part, rows, BY + 2 * RY)
    along = jnp.swapaxes(along, 1, 2).astype(jnp.bfloat16)
    wide_x = ramp_at(jnp.arange(BX + 2 * RX)[:, None] - starts_x[None, :], length) * active[None, :]
    wide_y = ramp_at(jnp.arange(BY + 2 * RY)[None, :] - starts_y[:, None], rows)
    wide_x = jnp.pad(wide_x, ((0, 0), (0, 16 - slots))).astype(jnp.bfloat16)
    wide_y = jnp.pad(wide_y, ((0, 16 - slots), (0, 0))).astype(jnp.bfloat16)
    return merged(grid_x, grid_y, depth_part, source_tiles, across, along, wide_x, wide_y)


def solution(mesh):
    placed = (
        P(("gx", "gy"), None, None, None),
        P(None, ("gx", "gy")),
        P(("gx", "gy")),
        P(("gx", "gy")),
    )
    return jax.shard_map(
        functools.partial(local, mesh.shape["gx"], mesh.shape["gy"]),
        mesh=mesh, in_specs=placed, out_specs=P(None, "gx", "gy"), check_vma=False,
    )
```

profile of v0, /device:TPU:12, one launch (start us, length us, event | category | flops | bytes accessed | tf_op | source)
XLA Modules:
  0.0 115.0 jit_solution(3514374193157047067)
XLA Ops:
  0.7 0.8 add_bitcast_fusion
  1.4 1.2 %broadcast_subtract_fusion = (f32[3]{0:T(128)S(1)}, f32[3]{0:T(128)S(1)}, f32[3]{0:T(128)}, f32[3]{0:T(128)S(1)}, f32[3]{0:T(128)S(1)}) fusion(s32[3]{0:T(128)} %param.6), kind=kLoop, calls=%fused_computation.55 | loop fusion | flops 177 | bytes 72 | tf_op jit(solution)/shard_map/sub | solution.py:30
  2.7 0.1 minimum_select_fusion.1
  2.8 0.1 iota_subtract_fusion.2
  2.8 0.1 fusion.6
  2.9 0.6 pad.11.wide_y_ref
  3.5 0.1 iota_subtract_fusion.1
  3.6 0.1 multiply_convert_fusion.1
  3.7 0.6 pad.10.wide_x_ref
  4.3 0.4 multiply_multiply_fusion
  4.7 1.1 concatenate.4.across_ref
  5.9 1.8 %multiply_convert_fusion.along_ref = bf16[3,384,512]{2,1,0:T(8,128)(2,1)} fusion(f32[3]{0:T(128)S(1)} %get-tuple-element.6, s32[3,512]{1,0:T(4,128)S(1)} %get-tuple-element.17, f32[3]{0:T(128)S(1)} %get-tuple-element.5, s32[3,512]{1,0:T(4,128)S(1)} %get-tuple-element.16, f32[3,512]{1,0:T(4,128)S(1)} %get-tuple-element.15), kind=kLoop, calls=%fused_computation | loop fusion | flops 4128768 | bytes 1198104 | tf_op jit(solution)/shard_map/convert_element_type | solution.py:236
  7.6 102.7 %merged.1 = f32[32,128,256]{2,1,0:T(8,128)} custom-call(f32[3]{0:T(128)} %get-tuple-element.18.depth_ref, bf16[3,32,192,384]{3,2,1,0:T(8,128)(2,1)} %next_ref.1, bf16[3,32,192,384]{3,2,1,0:T(8,128)(2,1)} %next_ref.1, bf16[256,1152]{1,0:T(8,128)(2,1)} %concatenate.4.across_ref, bf16[3,384,512]{2,1,0:T(8,128)(2,1)} %multiply_convert_fusion.along_ref, ...), custom_call_target="tpu_custom_call" | custom-call | tf_op jit(solution)/shard_map/merged/pallas_call | solution.py:189
  110.4 4.7 %copy.8 = f32[32,128,256]{2,1,0:T(8,128)} copy(f32[32,128,256]{2,1,0:T(8,128)} %merged.1) | data formatting | bytes 8388608
  (2 shorter events, 0.0 us)
where the time goes:
time: 116 us; the launch traced here: 115 us
  Pallas kernels  103 us (89%)
  local copies, waits for them, and re-layouts  7.07 us (6%)
  other arithmetic  4.54 us (4%)
    pallas_call x1, Pallas kernels, merged(): pl.pallas_call(functools.partial(kernel, grid_x, grid_y), grid=(count + L...  103 us
    unnamed x1, local copies, waits for them, and re-layouts  4.66 us

commit v1 on v0

v1 whole, which is shorter than its diff:
```python
import functools

import jax
import jax.numpy as jnp
from jax import lax
from jax.experimental import pallas as pl
from jax.experimental.pallas import tpu as pltpu
from jax.sharding import PartitionSpec as P

BX = 128
BY = 256
RAMP = 32
RX = 64
RY = 128
LAG_Y = 2
LAG_RELAY = 6
LAG_X = 12
LANES = 128
MESH = pl.DeviceIdType.MESH


def ramp_at(place, length):
    place = place.astype(jnp.float32)
    ramp = jnp.minimum(jnp.minimum(place + 1.0, length - place), float(RAMP))
    return jnp.maximum(ramp, 0.0)


def whole_iota(shape, dimension):
    return lax.broadcasted_iota(jnp.int32, shape, dimension)


def pick(index, options):
    chosen = options[-1]
    for number in range(len(options) - 2, -1, -1):
        chosen = jnp.where(index == number, options[number], chosen)
    return chosen


def kernel(
    grid_x, grid_y, offsets_ref, shifts_ref, counts_ref, first_ref, next_ref,
    out_ref, centre, up, down, above, below, from_left, from_right, relay, places,
    across, along, held, parts, scale,
    up_sent, down_sent, left_sent, right_sent, above_sem, below_sem, from_left_sem, from_right_sem,
    relay_sent, relay_sem, place_sent, place_sem,
):
    slots, length, rows = first_ref.shape[0], first_ref.shape[2], first_ref.shape[3]
    extent_x, extent_y = across.shape[0], along.shape[2]
    half = extent_y // 2
    count = centre.shape[0]
    pairs = grid_x // 2
    step = pl.program_id(0)
    column, row = lax.axis_index("gx"), lax.axis_index("gy")
    even = column % 2 == 0
    pair = column // 2
    has_left, has_right = column > 0, column < grid_x - 1
    has_below, has_above = row > 0, row < grid_y - 1
    far_left, far_right = column > 1, column < grid_x - 2
    to_left, to_right = (column - 1, row), (column + 1, row)
    to_below, to_above = (column, row - 1), (column, row + 1)
    to_far_left, to_far_right = (column - 2, row), (column + 2, row)

    def remote(source, target, sent, arrived, device):
        return pltpu.make_async_remote_copy(
            src_ref=source, dst_ref=target, send_sem=sent, recv_sem=arrived,
            device_id=device, device_id_type=MESH,
        )

    def copy_below(n):
        return remote(up.at[n], above.at[n], up_sent.at[n], above_sem.at[n], to_below)

    def copy_above(n):
        return remote(down.at[n], below.at[n], down_sent.at[n], below_sem.at[n], to_above)

    left_strip, right_strip = pl.ds(0, RX), pl.ds(RX + BX, RX)

    def copy_left(n):
        return remote(
            centre.at[n, left_strip], from_right.at[n], left_sent.at[n], from_right_sem.at[n], to_left
        )

    def copy_right(n):
        return remote(
            centre.at[n, right_strip], from_left.at[n], right_sent.at[n], from_left_sem.at[n], to_right
        )

    def detour_left(n):
        return remote(
            centre.at[n, left_strip], relay.at[n], left_sent.at[n], relay_sem.at[n], to_right
        )

    def detour_right(n):
        return remote(
            centre.at[n, right_strip], relay.at[n], right_sent.at[n], relay_sem.at[n], to_left
        )

    def relay_left(n):
        return remote(relay.at[n], from_right.at[n], relay_sent.at[n], from_right_sem.at[n], to_far_left)

    def relay_right(n):
        return remote(relay.at[n], from_left.at[n], relay_sent.at[n], from_left_sem.at[n], to_far_right)

    def by_relay_right(n):
        return n % pairs < pairs - 1 - pair

    def by_relay_left(n):
        return n % pairs < pair

    def place_copy(first, size, target, number, device):
        return remote(
            places.at[pl.ds(first, size)], places.at[pl.ds(target, size)],
            place_sent.at[number], place_sem.at[number], device,
        )

    place_above = place_copy(0, 1, 1, 0, to_above)
    place_below = place_copy(0, 1, 2, 1, to_below)
    place_right = place_copy(0, 3, 3, 2, to_right)
    place_left = place_copy(0, 3, 6, 3, to_left)

    def along_rows(plane, k):
        low = jnp.dot(plane, along[k, :, :half], preferred_element_type=jnp.float32)
        cut = half - RY
        high = jnp.dot(plane[:, cut:], along[k, cut:, half:], preferred_element_type=jnp.float32)
        return low, high

    @pl.when(step == 0)
    def _():
        barrier = pltpu.get_barrier_semaphore()
        peers = (
            (has_left, to_left), (has_right, to_right), (has_below, to_below), (has_above, to_above),
            (far_left, to_far_left), (far_right, to_far_right),
        )
        for there, device in peers:
            @pl.when(there)
            def _():
                pl.semaphore_signal(barrier, inc=1, device_id=device, device_id_type=MESH)

        starts_x = [offsets_ref[0, k] - column * BX for k in range(slots)]
        starts_y = [offsets_ref[1, k] - row * BY for k in range(slots)]
        active = [jnp.where(k < counts_ref[0], 1.0, 0.0) for k in range(slots)]
        shape = places.shape[1:]
        lane, tile = whole_iota(shape, 1), whole_iota(shape, 0)
        record = jnp.zeros(shape, jnp.float32)
        for k in range(slots):
            values = (starts_x[k].astype(jnp.float32), starts_y[k].astype(jnp.float32), active[k])
            for place, value in enumerate(values):
                record = jnp.where((tile == k) & (lane == place), value, record)
        places[0] = record
        for number in range(1, places.shape[0]):
            there = (has_below, has_above, has_left, has_right)[
                number - 1 if number < 3 else number // 3 + 1
            ]

            @pl.when(jnp.logical_not(there))
            def _():
                places[number] = jnp.zeros(shape, jnp.float32)

        for k in range(slots):
            fraction = (shifts_ref[k] % 4).astype(jnp.float32) * 0.25
            target = whole_iota((1, extent_y), 1) - (starts_y[k] + RY)
            ramp = ramp_at(target, rows)
            source = whole_iota((rows, extent_y), 0)
            here = jnp.where(source == target, ramp * (1.0 - fraction), 0.0)
            after = jnp.where(
                source == jnp.minimum(target + 1, rows - 1), ramp * fraction, 0.0
            )
            along[k] = (here + after).astype(jnp.bfloat16)
        wide = 2 * slots * length
        number = whole_iota((1, wide), 1)
        part = number // length
        source = number - part * length
        part = part // 2
        fraction = pick(
            part, [(shifts_ref[k] // 4 % 4).astype(jnp.float32) * 0.25 for k in range(slots)]
        )
        weight = pick(part, active)
        target = whole_iota((extent_x, wide), 0) - pick(part, [start + RX for start in starts_x])
        here = jnp.where(source == target, 1.0 - fraction, 0.0)
        after = jnp.where(source == jnp.minimum(target + 1, length - 1), fraction, 0.0)
        across[...] = (ramp_at(target, length) * weight * (here + after)).astype(jnp.bfloat16)

        for k in range(slots):
            low, high = along_rows(first_ref[k, 0], k)
            held[k, :, :half] = low
            held[k, :, half:] = high
        pl.semaphore_wait(barrier, sum(jnp.where(there, 1, 0) for there, device in peers))

        @pl.when(has_above)
        def _():
            place_above.start()

        @pl.when(has_below)
        def _():
            place_below.start()

    @pl.when(step < count)
    def _():
        for k in range(slots):
            fraction = (shifts_ref[k] // 16 % 4).astype(jnp.float32) * 0.25
            for number, later in enumerate(along_rows(next_ref[k, 0], k)):
                lanes = slice(number * half, (number + 1) * half)
                mixed = held[k, :, lanes] * (1.0 - fraction) + later * fraction
                held[k, :, lanes] = later
                top = mixed.astype(jnp.bfloat16)
                rest = (mixed - top.astype(jnp.float32)).astype(jnp.bfloat16)
                parts[2 * k * length : (2 * k + 1) * length, lanes] = top
                parts[(2 * k + 1) * length : (2 * k + 2) * length, lanes] = rest
        total = jnp.dot(across[...], parts[...], preferred_element_type=jnp.float32)
        up[step] = total[:, :RY]
        centre[step] = total[:, RY : RY + BY]
        down[step] = total[:, RY + BY :]

        @pl.when(has_below)
        def _():
            copy_below(step).start()

        @pl.when(has_above)
        def _():
            copy_above(step).start()

    @pl.when(step == LAG_Y)
    def _():
        @pl.when(has_below)
        def _():
            place_above.wait_recv()

        @pl.when(has_above)
        def _():
            place_below.wait_recv()

        @pl.when(has_right)
        def _():
            place_right.start()

        @pl.when(has_left)
        def _():
            place_left.start()

    @pl.when((step >= LAG_Y) & (step < count + LAG_Y))
    def _():
        n = step - LAG_Y

        @pl.when(has_below)
        def _():
            copy_above(n).wait_recv()
            centre[n, :, :RY] += below[n]

        @pl.when(has_above)
        def _():
            copy_below(n).wait_recv()
            centre[n, :, RY:] += above[n]

        detours_left = even & by_relay_left(n)
        detours_right = jnp.logical_not(even) & by_relay_right(n)

        @pl.when(has_left & detours_left)
        def _():
            detour_left(n).start()

        @pl.when(has_left & jnp.logical_not(detours_left))
        def _():
            copy_left(n).start()

        @pl.when(has_right & detours_right)
        def _():
            detour_right(n).start()

        @pl.when(has_right & jnp.logical_not(detours_right))
        def _():
            copy_right(n).start()

    @pl.when((step >= LAG_RELAY) & (step < count + LAG_RELAY))
    def _():
        n = step - LAG_RELAY

        @pl.when(even & far_right & by_relay_right(n))
        def _():
            detour_right(n).wait_recv()
            relay_right(n).start()

        @pl.when(jnp.logical_not(even) & far_left & by_relay_left(n))
        def _():
            detour_left(n).wait_recv()
            relay_left(n).start()

    @pl.when(step == LAG_X)
    def _():
        for there, copy in ((has_above, place_above), (has_below, place_below)):
            @pl.when(there)
            def _():
                copy.wait_send()

        @pl.when(has_left)
        def _():
            place_right.wait_recv()
            place_left.wait_send()

        @pl.when(has_right)
        def _():
            place_left.wait_recv()
            place_right.wait_send()

        total = jnp.zeros((BX, BY), jnp.float32)
        cell_x = whole_iota((BX, 1), 0).astype(jnp.float32)
        cell_y = whole_iota((1, BY), 1).astype(jnp.float32)
        for number in range(places.shape[0]):
            origin_x = float((0, -BX, BX)[number // 3])
            origin_y = float((0, -BY, BY)[number % 3])
            for k in range(slots):
                start_x = places[number, k : k + 1, 0:1] + origin_x
                start_y = places[number, k : k + 1, 1:2] + origin_y
                weight = places[number, k : k + 1, 2:3]
                total += (ramp_at(cell_x - start_x, length) * weight) * ramp_at(cell_y - start_y, rows)
        scale[...] = 1.0 / jnp.maximum(total, 1.0)

    @pl.when(step >= LAG_X)
    def _():
        n = step - LAG_X

        @pl.when(has_left)
        def _():
            copy_right(n).wait_recv()
            centre[n, RX : 2 * RX] += from_left[n]
            copy_left(n).wait_send()

        @pl.when(has_right)
        def _():
            copy_left(n).wait_recv()
            centre[n, BX : BX + RX] += from_right[n]
            copy_right(n).wait_send()

        @pl.when(has_below)
        def _():
            copy_below(n).wait_send()

        @pl.when(has_above)
        def _():
            copy_above(n).wait_send()

        @pl.when(even & far_right & by_relay_right(n))
        def _():
            relay_right(n).wait_send()

        @pl.when(jnp.logical_not(even) & far_left & by_relay_left(n))
        def _():
            relay_left(n).wait_send()

        out_ref[0] = centre[n, RX : RX + BX] * scale[...]


def local(grid_x, grid_y, tiles, tile_offsets, tile_shifts, tile_counts):
    slots, count, length, rows = tiles.shape
    extent_x, extent_y = BX + 2 * RX, BY + 2 * RY
    plane = (slots, 1, length, rows)
    slab = lambda *shape: pltpu.VMEM((count,) + shape, jnp.float32)
    return pl.pallas_call(
        functools.partial(kernel, grid_x, grid_y),
        grid=(count + LAG_X,),
        in_specs=[
            pl.BlockSpec(memory_space=pltpu.SMEM),
            pl.BlockSpec(memory_space=pltpu.SMEM),
            pl.BlockSpec(memory_space=pltpu.SMEM),
            pl.BlockSpec(plane, lambda s: (0, 0, 0, 0)),
            pl.BlockSpec(plane, lambda s: (0, jnp.minimum(s + 1, count - 1), 0, 0)),
        ],
        out_specs=pl.BlockSpec((1, BX, BY), lambda s: (jnp.maximum(s - LAG_X, 0), 0, 0)),
        out_shape=jax.ShapeDtypeStruct((count, BX, BY), jnp.float32),
        scratch_shapes=[
            slab(extent_x, BY),
            slab(extent_x, RY),
            slab(extent_x, RY),
            slab(extent_x, RY),
            slab(extent_x, RY),
            slab(RX, BY),
            slab(RX, BY),
            slab(RX, BY),
            pltpu.VMEM((9, 8 * pl.cdiv(slots, 8), LANES), jnp.float32),
            pltpu.VMEM((extent_x, 2 * slots * length), jnp.bfloat16),
            pltpu.VMEM((slots, rows, extent_y), jnp.bfloat16),
            pltpu.VMEM((slots, length, extent_y), jnp.float32),
            pltpu.VMEM((2 * slots * length, extent_y), jnp.bfloat16),
            pltpu.VMEM((BX, BY), jnp.float32),
        ]
        + [pltpu.SemaphoreType.DMA((count,))] * 10
        + [pltpu.SemaphoreType.DMA((4,))] * 2,
        compiler_params=pltpu.CompilerParams(
            collective_id=0, has_side_effects=True, vmem_limit_bytes=60 * 1024 * 1024,
            dimension_semantics=("arbitrary",),
        ),
        name="merged",
    )(tile_offsets, tile_shifts, tile_counts, tiles, tiles)


def solution(mesh):
    placed = (
        P(("gx", "gy"), None, None, None),
        P(None, ("gx", "gy")),
        P(("gx", "gy")),
        P(("gx", "gy")),
    )
    return jax.shard_map(
        functools.partial(local, mesh.shape["gx"], mesh.shape["gy"]),
        mesh=mesh, in_specs=placed, out_specs=P(None, "gx", "gy"), check_vma=False,
    )
```

time: 116 us -> 99.5 us (0.86)
  Pallas kernels: 103 us -> 92.4 us
  other arithmetic: 4.54 us -> 0 us
  local copies, waits for them, and re-layouts: 7.07 us -> 4.66 us
    pallas_call x1, Pallas kernels: 103 us -> 92.4 us  [local(): pl.pallas_call(functools.partial(kernel, grid_x, grid_y), grid=(count + L...]
    convert_element_type x2 -> x0, other arithmetic: 1.79 us -> none  [the longest x1 1.78 us: local(): along = jnp.swapaxes(along, 1, 2).astype(jnp.bfloat16)]
    sub x3 -> x0, other arithmetic: 1.39 us -> none  [the longest x1 1.25 us: band(): here = jnp.where(source == target, 1.0 - fraction, 0.0)]
    pad x2 -> x0, local copies, waits for them, and re-layouts: 1.24 us -> none  [the longest x1 0.63 us: local(): wide_x = jnp.pad(wide_x, ((0, 0), (0, 16 - slots))).astype(jnp.bfloat16)]
where the time goes in v1:
time: 99.5 us; the launch traced here: 97.7 us
  Pallas kernels  92.4 us (93%)
  local copies, waits for them, and re-layouts  4.66 us (5%)
    pallas_call x1, Pallas kernels, local(): pl.pallas_call(functools.partial(kernel, grid_x, grid_y), grid=(count + L...  92.4 us
    unnamed x1, local copies, waits for them, and re-layouts  4.66 us

profile of v1, /device:TPU:12, one launch (start us, length us, event | category | flops | bytes accessed | tf_op | source)
XLA Modules:
  0.0 97.7 jit_solution(8960716500794611275)
XLA Ops:
  0.7 92.4 %merged.1 = f32[32,128,256]{2,1,0:T(8,128)} custom-call(s32[2,3]{1,0:T(2,128)} %offsets_ref.1, s32[3]{0:T(128)} %shifts_ref.1, s32[1]{0:T(128)S(6)} %copy.6.counts_ref, bf16[3,32,192,384]{3,2,1,0:T(8,128)(2,1)} %next_ref.1, bf16[3,32,192,384]{3,2,1,0:T(8,128)(2,1)} %next_ref.1), custom_call_target="tpu_custom_call" | custom-call | tf_op jit(solution)/shard_map/merged/pallas_call | solution.py:355
  93.1 4.7 %copy.7 = f32[32,128,256]{2,1,0:T(8,128)} copy(f32[32,128,256]{2,1,0:T(8,128)} %merged.1) | data formatting | bytes 8388608

commit v2 on v1

--- a/solution.py
+++ b/solution.py
@@ -12,8 +12,8 @@
 RAMP = 32
 RX = 64
 RY = 128
-LAG_Y = 2
-LAG_RELAY = 6
+LAG_Y = 1
+LAG_RELAY = 5
 LAG_X = 12
 LANES = 128
 MESH = pl.DeviceIdType.MESH
@@ -344,7 +344,7 @@
         def _():
             relay_left(n).wait_send()
 
-        out_ref[0] = centre[n, RX : RX + BX] * scale[...]
+        out_ref[n] = centre[n, RX : RX + BX] * scale[...]
 
 
 def local(grid_x, grid_y, tiles, tile_offsets, tile_shifts, tile_counts):
@@ -362,8 +362,8 @@
             pl.BlockSpec(plane, lambda s: (0, 0, 0, 0)),
             pl.BlockSpec(plane, lambda s: (0, jnp.minimum(s + 1, count - 1), 0, 0)),
         ],
-        out_specs=pl.BlockSpec((1, BX, BY), lambda s: (jnp.maximum(s - LAG_X, 0), 0, 0)),
-        out_shape=jax.ShapeDtypeStruct((count, BX, BY), jnp.float32),
+        out_specs=pl.BlockSpec(memory_space=pltpu.VMEM),
+        out_shape=pltpu.VMEM((count, BX, BY), jnp.float32),
         scratch_shapes=[
             slab(extent_x, BY),
             slab(extent_x, RY),
@@ -383,7 +383,7 @@
         + [pltpu.SemaphoreType.DMA((count,))] * 10
         + [pltpu.SemaphoreType.DMA((4,))] * 2,
         compiler_params=pltpu.CompilerParams(
-            collective_id=0, has_side_effects=True, vmem_limit_bytes=60 * 1024 * 1024,
+            collective_id=0, has_side_effects=True, vmem_limit_bytes=52 * 1024 * 1024,
             dimension_semantics=("arbitrary",),
         ),
         name="merged",

time: 99.5 us -> 94.2 us (0.947); the launches traced: 97.7 us -> 94 us
  local copies, waits for them, and re-layouts: 4.66 us -> 2.02 us
  Pallas kernels: 92.4 us -> 91.3 us
    unnamed x1, local copies, waits for them, and re-layouts: 4.66 us -> 2.02 us
    pallas_call x1, Pallas kernels: 92.4 us -> 91.3 us  [local(): pl.pallas_call(functools.partial(kernel, grid_x, grid_y), grid=(count + L...]
where the time goes in v2:
time: 94.2 us; the launch traced here: 94 us
  Pallas kernels  91.3 us (97%)
  local copies, waits for them, and re-layouts  2.02 us (2%)
    pallas_call x1, Pallas kernels, local(): pl.pallas_call(functools.partial(kernel, grid_x, grid_y), grid=(count + L...  91.3 us
    unnamed x1, local copies, waits for them, and re-layouts  2.02 us

profile of v2, /device:TPU:12, one launch (start us, length us, event | category | flops | bytes accessed | tf_op | source)
XLA Modules:
  0.0 94.0 jit_solution(6214970578718407796)
XLA Ops:
  0.7 91.3 %merged.1 = f32[32,128,256]{2,1,0:T(8,128)S(1)} custom-call(s32[2,3]{1,0:T(2,128)} %offsets_ref.1, s32[3]{0:T(128)} %shifts_ref.1, s32[1]{0:T(128)S(6)} %copy.7.counts_ref, bf16[3,32,192,384]{3,2,1,0:T(8,128)(2,1)} %next_ref.1, bf16[3,32,192,384]{3,2,1,0:T(8,128)(2,1)} %next_ref.1), custom_call_target="tpu_custom_call" | custom-call | tf_op jit(solution)/shard_map/merged/pallas_call | solution.py:355
  92.0 2.0 %copy.6 = f32[32,128,256]{2,1,0:T(8,128)} copy(f32[32,128,256]{2,1,0:T(8,128)S(1)} %merged.1) | data formatting | bytes 8388608

commit v3 on v2

--- a/solution.py
+++ b/solution.py
@@ -27,13 +27,6 @@
 
 def whole_iota(shape, dimension):
     return lax.broadcasted_iota(jnp.int32, shape, dimension)
-
-
-def pick(index, options):
-    chosen = options[-1]
-    for number in range(len(options) - 2, -1, -1):
-        chosen = jnp.where(index == number, options[number], chosen)
-    return chosen
 
 
 def kernel(
@@ -164,19 +157,18 @@
                 source == jnp.minimum(target + 1, rows - 1), ramp * fraction, 0.0
             )
             along[k] = (here + after).astype(jnp.bfloat16)
-        wide = 2 * slots * length
-        number = whole_iota((1, wide), 1)
-        part = number // length
-        source = number - part * length
-        part = part // 2
-        fraction = pick(
-            part, [(shifts_ref[k] // 4 % 4).astype(jnp.float32) * 0.25 for k in range(slots)]
-        )
-        weight = pick(part, active)
-        target = whole_iota((extent_x, wide), 0) - pick(part, [start + RX for start in starts_x])
-        here = jnp.where(source == target, 1.0 - fraction, 0.0)
-        after = jnp.where(source == jnp.minimum(target + 1, length - 1), fraction, 0.0)
-        across[...] = (ramp_at(target, length) * weight * (here + after)).astype(jnp.bfloat16)
+        for k in range(slots):
+            fraction = (shifts_ref[k] // 4 % 4).astype(jnp.float32) * 0.25
+            target = whole_iota((extent_x, 1), 0) - (starts_x[k] + RX)
+            ramp = ramp_at(target, length) * active[k]
+            source = whole_iota((extent_x, length), 1)
+            here = jnp.where(source == target, ramp * (1.0 - fraction), 0.0)
+            after = jnp.where(
+                source == jnp.minimum(target + 1, length - 1), ramp * fraction, 0.0
+            )
+            placed = (here + after).astype(jnp.bfloat16)
+            across[:, 2 * k * length : (2 * k + 1) * length] = placed
+            across[:, (2 * k + 1) * length : (2 * k + 2) * length] = placed
 
         for k in range(slots):
             low, high = along_rows(first_ref[k, 0], k)

time: 94.2 us -> 94.2 us (level)
  no operation moved by 1% of the time
where the time goes in v3:
time: 94.2 us; the launch traced here: 94 us
  Pallas kernels  91.3 us (97%)
  local copies, waits for them, and re-layouts  2.02 us (2%)
    pallas_call x1, Pallas kernels, local(): pl.pallas_call(functools.partial(kernel, grid_x, grid_y), grid=(count + L...  91.3 us
    unnamed x1, local copies, waits for them, and re-layouts  2.02 us

profile of v3, /device:TPU:12, one launch (start us, length us, event | category | flops | bytes accessed | tf_op | source)
XLA Modules:
  0.0 94.0 jit_solution(6958280090940189273)
XLA Ops:
  0.7 91.3 %merged.1 = f32[32,128,256]{2,1,0:T(8,128)S(1)} custom-call(s32[2,3]{1,0:T(2,128)} %offsets_ref.1, s32[3]{0:T(128)} %shifts_ref.1, s32[1]{0:T(128)S(6)} %copy.7.counts_ref, bf16[3,32,192,384]{3,2,1,0:T(8,128)(2,1)} %next_ref.1, bf16[3,32,192,384]{3,2,1,0:T(8,128)(2,1)} %next_ref.1), custom_call_target="tpu_custom_call" | custom-call | tf_op jit(solution)/shard_map/merged/pallas_call | solution.py:347
  92.0 2.0 %copy.6 = f32[32,128,256]{2,1,0:T(8,128)} copy(f32[32,128,256]{2,1,0:T(8,128)S(1)} %merged.1) | data formatting | bytes 8388608
